TPU v7x, 32 devices: a whole 2x2x4 slice. The times are simulated.
32 devices in a mesh: seq: 16 (over z, y, core), head: 2 (over x).
Axes of the slice: x: 2, y: 2, z: 4, core: 2. Of those that a mesh axis runs over, the one named last changes fastest.
Arguments:
- teacher: bfloat16 [1, 4096, 4096], P(None, 'seq', 'head'), may hold values from -32 to 32
- student: bfloat16 [1, 4096, 1792], P(None, 'seq', 'head'), may hold values from -32 to 32
- weights: float32 [4096], P('seq'), may hold values from 1 to 32
Outputs:
- mean_loss: float32 [], replicated
- student_grad: float32 [1, 4096, 1792], P(None, 'seq', 'head')
All inputs are finite; a program needn't handle non-finite values.
Results may differ from a plain program's by a relative error of at most 0.0011.
Values may be sent and summed in bfloat16 or wider, within the bound.
A program may use at most 128 MiB of HBM per device.

v0:
```python
import math
import jax
import jax.numpy as jnp
from jax import lax
from jax.sharding import PartitionSpec as P

TW = 256
SW = 112
HEADS = 16


def relation_scores(own_rows, key_piece, head_size):
    relations, tok_rows, columns = own_rows.shape
    head_count = columns // head_size
    queries = own_rows.reshape(relations, tok_rows, head_count, head_size)
    keys_split = key_piece.reshape(relations, key_piece.shape[1], head_count, head_size)
    return jnp.einsum(
        "rihd,rjhd->rhij", queries, keys_split, preferred_element_type=jnp.float32
    ) * (1.0 / math.sqrt(head_size))


def local(teacher, student, weights):
    relations, tok_rows, columns = teacher.shape
    head_count = columns // TW
    cycle_size = lax.axis_size("seq")
    lowest = jnp.full((relations, head_count, tok_rows), -jnp.inf, jnp.float32)
    zeroes = jnp.zeros((relations, head_count, tok_rows), jnp.float32)
    pieces = (
        lax.all_gather(teacher, "seq", axis=1, tiled=True),
        lax.all_gather(student, "seq", axis=1, tiled=True),
    )
    teach_max = lowest
    teach_sum = zeroes
    teach_cross = zeroes
    stud_max = lowest
    stud_sum = zeroes
    teach_score = relation_scores(teacher, pieces[0], TW)
    stud_score = relation_scores(student, pieces[1], SW)
    teach_top = jnp.max(teach_score, axis=-1)
    stud_top = jnp.max(stud_score, axis=-1)
    teach_exp = jnp.exp(teach_score - teach_top[..., None])
    stud_exp = jnp.exp(stud_score - stud_top[..., None])
    teach_keep = jnp.exp(teach_max - teach_top)
    stud_keep = jnp.exp(stud_max - stud_top)
    sweep_stats = (
        teach_top,
        teach_sum * teach_keep + jnp.sum(teach_exp, axis=-1),
        teach_cross * teach_keep + jnp.sum(teach_exp * (teach_score - stud_score), axis=-1),
        stud_top,
        stud_sum * stud_keep + jnp.sum(stud_exp, axis=-1),
    )
    teach_max, teach_sum, teach_cross, stud_max, stud_sum = sweep_stats
    teach_norm = teach_max + jnp.log(teach_sum)
    stud_norm = stud_max + jnp.log(stud_sum)
    divergence = teach_cross / teach_sum - teach_norm + stud_norm
    partial_loss = jnp.sum(weights[None, None, :] * divergence)
    loss_sum = lax.psum(partial_loss, ("seq", "head"))
    mean_loss = loss_sum / (relations * HEADS * tok_rows * cycle_size)
    every_teach, every_stud, every_weight = (
        lax.all_gather(teach_norm, "seq", axis=2, tiled=True),
        lax.all_gather(stud_norm, "seq", axis=2, tiled=True),
        lax.all_gather(weights, "seq", axis=0, tiled=True),
    )
    pieces = (
        lax.all_gather(teacher, "seq", axis=1, tiled=True),
        lax.all_gather(student, "seq", axis=1, tiled=True),
    )
    key_count = pieces[0].shape[1]
    teach_score = relation_scores(teacher, pieces[0], TW)
    stud_score = relation_scores(student, pieces[1], SW)
    row_part = weights[None, None, :, None] * (
        jnp.exp(stud_score - stud_norm[..., None]) - jnp.exp(teach_score - teach_norm[..., None])
    )
    col_part = every_weight[None, None, None, :] * (
        jnp.exp(stud_score - every_stud[:, :, None, :])
        - jnp.exp(teach_score - every_teach[:, :, None, :])
    )
    slope_mix = (row_part + col_part).astype(jnp.bfloat16)
    stud_keys = pieces[1].reshape(relations, key_count, head_count, SW)
    summed = jnp.einsum("rhij,rjhd->rihd", slope_mix, stud_keys, preferred_element_type=jnp.float32)
    student_grad = (summed * (1.0 / math.sqrt(SW))).reshape(relations, tok_rows, head_count * SW)
    return (mean_loss, student_grad)


def solution(mesh):
    return jax.shard_map(
        local,
        mesh=mesh,
        in_specs=(P(None, "seq", "head"), P(None, "seq", "head"), P("seq")),
        out_specs=(P(), P(None, "seq", "head")),
        check_vma=False,
    )
```

profile of v0, /device:TPU:0, one launch (start us, length us, event | category | flops | bytes accessed | tf_op | source)
XLA Modules:
  0.0 392.5 jit_solution(11814815298845756084)
XLA Ops:
  7.2 0.0 all-gather.6.cloned.1.call-start
  7.2 0.7 all-gather.6.cloned.1.call-update
  7.9 0.0 all-gather.4.cloned.1.call-start
  7.9 2.3 copy.15
  10.2 0.0 all-gather.4.cloned.1.call-update
  10.2 1.2 copy.18
  11.5 1.5 copy.22
  13.0 23.6 %all-gather = f32[16,1,256]{2,1,0:T(1,128)S(1)} all-gather(f32[1,1,256]{2,1,0:T(1,128)} %bitcast.61), channel_id=1, replica_groups=mesh['seq'=16,'head'=2] {'seq'}, dimensions={0}, use_global_device_ids=true | all-gather | bytes 17408 | tf_op jit(solution)/shard_map/all_gather | solution.py:62
  36.6 44.1 %all-gather.6.cloned.1.call-done = bf16[1,4096,896]{2,1,0:T(8,128)(2,1)} async-done(((bf16[1,256,896]{2,1,0:T(8,128)(2,1)}), bf16[1,4096,896]{2,1,0:T(8,128)(2,1)}) %all-gather.6.cloned.1.call-update) | async-done | bytes 7340048 | tf_op jit(solution)/shard_map/all_gather | solution.py:30
  80.7 10.8 %copy.19 = bf16[1,4096,896]{1,2,0:T(8,128)(2,1)} copy(bf16[1,4096,896]{2,1,0:T(8,128)(2,1)} %all-gather.6.cloned.1.call-done) | data formatting | bytes 14680064 | tf_op jit(solution)/shard_map/all_gather | solution.py:30
  91.5 120.0 %all-gather.4.cloned.1.call-done = bf16[1,4096,2048]{1,2,0:T(8,128)(2,1)} async-done(((bf16[1,256,2048]{1,2,0:T(8,128)(2,1)}), bf16[1,4096,2048]{1,2,0:T(8,128)(2,1)}) %all-gather.4.cloned.1.call-update) | async-done | bytes 16777232 | tf_op jit(solution)/shard_map/all_gather | solution.py:29
  211.6 19.3 %multiply_reduce_fusion.2 = (f32[8,256]{1,0:T(8,128)S(1)}, f32[8,256,4096]{2,1,0:T(8,128)}) fusion(bf16[4096,8,256]{0,2,1:T(8,128)(2,1)} %bitcast.51, bf16[256,8,256]{2,1,0:T(8,128)(2,1)S(1)} %bitcast.54), kind=kOutput, calls=%fused_computation.6 | convolution fusion | flops 4311742464 | bytes 51388416 | tf_op jit(solution)/shard_map/rihd,rjhd->rhij/dot_general | solution.py:17
  230.8 29.6 %fusion = (f32[8,256]{1,0:T(8,128)S(1)}, f32[8,256]{1,0:T(8,128)S(1)}, f32[8,256]{1,0:T(8,128)S(1)}, f32[8,256,4096]{2,1,0:T(8,128)}) fusion(f32[8,256,4096]{2,1,0:T(8,128)} %get-tuple-element.15, f32[8,256]{1,0:T(8,128)S(1)} %get-tuple-element.14, bf16[256,8,112]{0,2,1:T(8,128)(2,1)S(1)} %bitcast.57, bf16[4096,8,112]{0,2,1:T(8,128)(2,1)} %bitcast.52), kind=kOutput, calls=%fused_computation.4 | convolution fusion | flops 1946150912 | bytes 74940416 | tf_op jit(solution)/shard_map/rihd,rjhd->rhij/dot_general | solution.py:17
  260.5 0.0 copy-start
  260.5 14.0 %exponential_reduce_fusion = f32[8,256]{1,0:T(8,128)S(1)} fusion(f32[8,256,4096]{2,1,0:T(8,128)} %get-tuple-element.16, f32[8,256]{1,0:T(8,128)S(1)} %get-tuple-element.10), kind=kLoop, calls=%fused_computation.1 | loop fusion | flops 25163776 | bytes 33570816 | tf_op jit(solution)/shard_map/reduce_sum | solution.py:50
  274.5 0.0 copy-done
  274.6 0.6 multiply_reduce_fusion.3
  275.2 38.5 %psum.7 = f32[]{:T(128)} all-reduce(f32[]{:T(128)} %get-tuple-element.11), channel_id=1, replica_groups=mesh['seq'=16,'head'=2] {'seq','head'}, use_global_device_ids=true, to_apply=%region_6.0 | all-reduce | flops 1 | bytes 8 | tf_op jit(solution)/shard_map/psum | solution.py:57
  313.7 21.6 %all_gather.21 = f32[1,8,4096]{2,1,0:T(8,128)S(1)} all-gather(f32[1,8,256]{2,1,0:T(8,128)S(1)} %fusion.6), channel_id=1, replica_groups=mesh['seq'=16,'head'=2] {'seq'}, dimensions={2}, use_global_device_ids=true | all-gather | bytes 139264 | tf_op jit(solution)/shard_map/all_gather | solution.py:60
  335.3 17.9 %all_gather.20 = f32[1,8,4096]{2,1,0:T(8,128)S(1)} all-gather(f32[1,8,256]{2,1,0:T(8,128)S(1)} %fusion.10), channel_id=1, replica_groups=mesh['seq'=16,'head'=2] {'seq'}, dimensions={2}, use_global_device_ids=true | all-gather | bytes 139264 | tf_op jit(solution)/shard_map/all_gather | solution.py:61
  353.2 29.4 %fusion.2 = f32[8,256,112]{1,2,0:T(8,128)S(1)} fusion(bf16[4096,8,112]{0,2,1:T(8,128)(2,1)} %bitcast.53, f32[8,256,4096]{2,1,0:T(8,128)} %get-tuple-element.16, f32[8,256,4096]{2,1,0:T(8,128)} %get-tuple-element.15, f32[8,4096]{1,0:T(8,128)S(1)} %bitcast.58, f32[8,4096]{1,0:T(8,128)S(1)} %bitcast.59, f32[4096]{0:T(1024)S(1)} %bitcast.60, ...), kind=kOutput, calls=%fused_computation.8 | convolution fusion | flops 1979940864 | bytes 75662336 | tf_op jit(solution)/shard_map/rhij,rjhd->rihd/dot_general | solution.py:80
  382.7 1.2 copy.20
  (2 shorter events, 0.0 us)
Async XLA Ops:
  7.2 73.6 %all-gather.6.cloned.1.call-start = ((), (), s32[]{:S(2)}) async-start(), calls=%async_computation.1 | async-start | bytes 7798784 | tf_op jit(solution)/shard_map/all_gather | solution.py:30
  7.9 203.7 %all-gather.4.cloned.1.call-start = ((), (), s32[]{:S(2)}) async-start(), calls=%async_computation | async-start | bytes 17825792 | tf_op jit(solution)/shard_map/all_gather | solution.py:29
  260.5 14.1 %copy-start = (f32[256]{0:T(256)S(1)}, f32[256]{0:T(256)}, u32[]{:S(2)}) copy-start(f32[256]{0:T(256)} %param.5) | copy-start | bytes 3076
Sparse Core Ops, SparseCore 0:
  10.3 70.4 all-gather.5
  82.9 128.6 all-gather.3
where the time goes:
time: 393 us
  waiting for transfers between devices  165 us (42%)
  blocking collectives  102 us (26%)
  matrix products  78.3 us (20%)
  local copies, waits for them, and re-layouts  17.1 us (4%)
  between operations  15.9 us (4%)
  other arithmetic  14.7 us (4%)
    all_gather x1, waiting for transfers between devices, local(): lax.all_gather(teacher, 'seq', axis=1, tiled=True)  120 us
    dot_general x2, matrix products, relation_scores(): jnp.einsum('rihd,rjhd->rhij', queries, keys_split, preferred_element_type...  48.9 us
    all_gather x1, waiting for transfers between devices, local(): lax.all_gather(student, 'seq', axis=1, tiled=True)  44.1 us
    psum x1, blocking collectives, local(): loss_sum = lax.psum(partial_loss, ('seq', 'head'))  38.5 us
    dot_general x1, matrix products, local(): jnp.einsum('rhij,rjhd->rihd', slope_mix, stud_keys, preferred_element_typ...  29.4 us
    all_gather x1, blocking collectives, local(): lax.all_gather(weights, 'seq', axis=0, tiled=True)  23.6 us
    all_gather x1, blocking collectives, local(): lax.all_gather(teach_norm, 'seq', axis=2, tiled=True)  21.6 us
    all_gather x1, blocking collectives, local(): lax.all_gather(stud_norm, 'seq', axis=2, tiled=True)  17.9 us
  transfers between devices with their start and end apart: 2, of which 2 were waited for; matrix products, arithmetic and copies ran while one was open for 4% of the time, Pallas kernels for 0%

commit v1 on v0

--- a/solution.py
+++ b/solution.py
@@ -26,7 +26,7 @@
     lowest = jnp.full((relations, head_count, tok_rows), -jnp.inf, jnp.float32)
     zeroes = jnp.zeros((relations, head_count, tok_rows), jnp.float32)
     pieces = (
-        lax.all_gather(teacher, "seq", axis=1, tiled=True),
+        jnp.concatenate(lax.all_gather(teacher, "seq"), axis=1),
         lax.all_gather(student, "seq", axis=1, tiled=True),
     )
     teach_max = lowest

time: 393 us -> 424 us (1.079)
  local copies, waits for them, and re-layouts: 17.1 us -> 33.5 us
  matrix products: 78.3 us -> 93.8 us
    all_gather x1, waiting for transfers between devices: 120 us -> 0.01 us  [local(): lax.all_gather(teacher, 'seq', axis=1, tiled=True)]
    all_gather x0 -> x1, waiting for transfers between devices: none -> 117 us  [local(): lax.all_gather(teacher, 'seq')]
    unnamed x6 -> x7, local copies, waits for them, and re-layouts: 6.25 us -> 22.7 us
    dot_general x2, matrix products: 48.9 us -> 62 us  [relation_scores(): jnp.einsum('rihd,rjhd->rhij', queries, keys_split, preferred_element_type...]
  transfers between devices with their start and end apart: 2 -> 3, of which waited for: 2 -> 2; matrix products, arithmetic and copies ran while one was open for 4% -> 26% of each run, Pallas kernels for 0% -> 0%
where the time goes in v1:
time: 424 us; the launch traced here: 423 us
  waiting for transfers between devices  161 us (38%)
  blocking collectives  104 us (25%)
  matrix products  93.8 us (22%)
  local copies, waits for them, and re-layouts  33.5 us (8%)
  between operations  15.6 us (4%)
  other arithmetic  14.9 us (4%)
    all_gather x1, waiting for transfers between devices, local(): lax.all_gather(teacher, 'seq')  117 us
    dot_general x2, matrix products, relation_scores(): jnp.einsum('rihd,rjhd->rhij', queries, keys_split, preferred_element_type...  62 us
    all_gather x1, waiting for transfers between devices, local(): lax.all_gather(student, 'seq', axis=1, tiled=True)  43.2 us
    psum x1, blocking collectives, local(): loss_sum = lax.psum(partial_loss, ('seq', 'head'))  38.8 us
    dot_general x1, matrix products, local(): jnp.einsum('rhij,rjhd->rihd', slope_mix, stud_keys, preferred_element_typ...  31.8 us
    all_gather x1, blocking collectives, local(): lax.all_gather(weights, 'seq', axis=0, tiled=True)  23.8 us
    unnamed x7, local copies, waits for them, and re-layouts  22.7 us
    all_gather x1, blocking collectives, local(): lax.all_gather(teach_norm, 'seq', axis=2, tiled=True)  22.2 us
  transfers between devices with their start and end apart: 3, of which 2 were waited for; matrix products, arithmetic and copies ran while one was open for 26% of the time, Pallas kernels for 0%

profile of v1, /device:TPU:0, one launch (start us, length us, event | category | flops | bytes accessed | tf_op | source)
XLA Modules:
  0.0 423.3 jit_solution(6948077724405835987)
XLA Ops:
  7.2 0.0 all-gather.6.cloned.1.call-start
  7.2 0.7 all-gather.6.cloned.1.call-update
  7.9 0.0 all-gather.10.cloned.1.call-start
  7.9 0.7 all-gather.10.cloned.1.call-update
  8.6 0.0 all-gather.8.cloned.1.call-start
  8.7 2.3 copy.22
  11.0 0.0 all-gather.8.cloned.1.call-update
  11.0 1.2 copy.20
  12.2 1.5 copy.27
  13.8 23.8 %all-gather.1 = f32[16,1,256]{2,1,0:T(1,128)S(1)} all-gather(f32[1,1,256]{2,1,0:T(1,128)} %bitcast.66), channel_id=1, replica_groups=mesh['seq'=16,'head'=2] {'seq'}, dimensions={0}, use_global_device_ids=true | all-gather | bytes 17408 | tf_op jit(solution)/shard_map/all_gather | solution.py:62
  37.6 43.2 %all-gather.6.cloned.1.call-done = bf16[1,4096,896]{2,1,0:T(8,128)(2,1)} async-done(((bf16[1,256,896]{2,1,0:T(8,128)(2,1)}), bf16[1,4096,896]{2,1,0:T(8,128)(2,1)}) %all-gather.6.cloned.1.call-update) | async-done | bytes 7340048 | tf_op jit(solution)/shard_map/all_gather | solution.py:30
  80.7 10.8 %copy.21 = bf16[1,4096,896]{1,2,0:T(8,128)(2,1)} copy(bf16[1,4096,896]{2,1,0:T(8,128)(2,1)} %all-gather.6.cloned.1.call-done) | data formatting | bytes 14680064 | tf_op jit(solution)/shard_map/all_gather | solution.py:30
  91.5 116.6 %all-gather.10.cloned.1.call-done = bf16[16,256,2048]{2,1,0:T(8,128)(2,1)} async-done(((bf16[1,256,2048]{2,1,0:T(8,128)(2,1)}), bf16[16,256,2048]{2,1,0:T(8,128)(2,1)}) %all-gather.10.cloned.1.call-update) | async-done | bytes 16777232 | tf_op jit(solution)/shard_map/all_gather | solution.py:29
  208.1 16.4 %copy.28 = bf16[512,8,8,256]{3,2,1,0:T(8,128)(2,1)} copy(bf16[512,8,8,256]{3,1,2,0:T(8,128)(2,1)} %bitcast.55) | data formatting | bytes 33554432
  224.6 31.9 %multiply_reduce_fusion.1 = (f32[8,256]{1,0:T(8,128)S(1)}, f32[8,256,4096]{2,1,0:T(8,128)}) fusion(bf16[4096,8,256]{2,1,0:T(8,128)(2,1)} %bitcast.54, bf16[256,8,256]{2,1,0:T(8,128)(2,1)S(1)} %bitcast.59), kind=kOutput, calls=%fused_computation.5 | convolution fusion | flops 4311742464 | bytes 51388416 | tf_op jit(solution)/shard_map/rihd,rjhd->rhij/dot_general | solution.py:17
  256.4 30.1 %fusion = (f32[8,256]{1,0:T(8,128)S(1)}, f32[8,256]{1,0:T(8,128)S(1)}, f32[8,256]{1,0:T(8,128)S(1)}, f32[8,256,4096]{2,1,0:T(8,128)}) fusion(f32[8,256,4096]{2,1,0:T(8,128)} %get-tuple-element.15, f32[8,256]{1,0:T(8,128)S(1)} %get-tuple-element.14, bf16[256,8,112]{0,2,1:T(8,128)(2,1)S(1)} %bitcast.62, bf16[4096,8,112]{0,2,1:T(8,128)(2,1)} %bitcast.57), kind=kOutput, calls=%fused_computation.4 | convolution fusion | flops 1946150912 | bytes 74940416 | tf_op jit(solution)/shard_map/rihd,rjhd->rhij/dot_general | solution.py:17
  286.6 14.2 %exponential_reduce_fusion = f32[8,256]{1,0:T(8,128)S(1)} fusion(f32[8,256,4096]{2,1,0:T(8,128)} %get-tuple-element.16, f32[8,256]{1,0:T(8,128)S(1)} %get-tuple-element.10), kind=kLoop, calls=%fused_computation.1 | loop fusion | flops 25163776 | bytes 33570816 | tf_op jit(solution)/shard_map/reduce_sum | solution.py:50
  300.8 19.5 %all_gather.27 = f32[1,8,4096]{2,1,0:T(8,128)S(1)} all-gather(f32[1,8,256]{2,1,0:T(8,128)S(1)} %fusion.15), channel_id=1, replica_groups=mesh['seq'=16,'head'=2] {'seq'}, dimensions={2}, use_global_device_ids=true | all-gather | bytes 139264 | tf_op jit(solution)/shard_map/all_gather | solution.py:61
  320.3 22.2 %all_gather.28 = f32[1,8,4096]{2,1,0:T(8,128)S(1)} all-gather(f32[1,8,256]{2,1,0:T(8,128)S(1)} %fusion.11), channel_id=1, replica_groups=mesh['seq'=16,'head'=2] {'seq'}, dimensions={2}, use_global_device_ids=true | all-gather | bytes 139264 | tf_op jit(solution)/shard_map/all_gather | solution.py:60
  342.6 0.0 copy-done
  342.6 0.6 multiply_reduce_fusion.3
  343.2 31.8 %fusion.6 = f32[8,256,112]{1,2,0:T(8,128)S(1)} fusion(bf16[4096,8,112]{0,2,1:T(8,128)(2,1)} %bitcast.58, f32[8,256,4096]{2,1,0:T(8,128)} %get-tuple-element.16, f32[8,4096]{1,0:T(8,128)S(1)} %bitcast.64, f32[8,4096]{1,0:T(8,128)S(1)} %bitcast.63, f32[4096]{0:T(1024)S(1)} %bitcast.65, f32[8,256]{1,0:T(8,128)S(1)} %get-tuple-element.13, ...), kind=kOutput, calls=%fused_computation.11 | convolution fusion | flops 6274908160 | bytes 59933696 | tf_op jit(solution)/shard_map/rhij,rjhd->rihd/dot_general | solution.py:80
  375.0 1.2 copy.25
  376.2 38.8 %psum.7 = f32[]{:T(128)} all-reduce(f32[]{:T(128)} %get-tuple-element.11), channel_id=1, replica_groups=mesh['seq'=16,'head'=2] {'seq','head'}, use_global_device_ids=true, to_apply=%region_6.0 | all-reduce | flops 1 | bytes 8 | tf_op jit(solution)/shard_map/psum | solution.py:57
  (4 shorter events, 0.0 us)
Async XLA Ops:
  7.2 73.6 %all-gather.6.cloned.1.call-start = ((), (), s32[]{:S(2)}) async-start(), calls=%async_computation | async-start | bytes 7798784 | tf_op jit(solution)/shard_map/all_gather | solution.py:30
  7.9 200.2 %all-gather.10.cloned.1.call-start = ((), (), s32[]{:S(2)}) async-start(), calls=%async_computation.2 | async-start | bytes 17825792 | tf_op jit(solution)/shard_map/all_gather | solution.py:29
  8.6 334.5 %all-gather.8.cloned.1.call-start = ((), (), s32[]{:S(2)}) async-start(), calls=%async_computation.1 | async-start | bytes 17825792 | tf_op jit(solution)/shard_map/all_gather | solution.py:65
  286.6 56.0 %copy-start = (f32[256]{0:T(256)S(1)}, f32[256]{0:T(256)}, u32[]{:S(2)}) copy-start(f32[256]{0:T(256)} %param.5) | copy-start | bytes 3076
Sparse Core Ops, SparseCore 0:
  10.3 70.4 all-gather.5
  82.9 125.1 all-gather.9
  210.3 129.3 all-gather.7
